TPU v7x, 32 devices: a whole 2x2x4 slice. The times are simulated.
32 devices in a mesh: ens: 4 (over x, core), elem: 8 (over z, y).
Axes of the slice: x: 2, y: 2, z: 4, core: 2. Of those that a mesh axis runs over, the one named last changes fastest.
Arguments:
- scalars: float32 [8, 512, 1024], P('ens', None, 'elem'), parts along dimension 0, may hold values from -6 to 6
- transport: float32 [3, 512, 1024], P(None, None, 'elem'), may hold values from -6 to 6
- mass: float32 [512, 1024], P(None, 'elem'), may hold values from 0.5 to 2
- element_order: int32 [8, 128], P('elem'), may hold values from 0 to 127, each once within a row
Outputs:
- advected: float32 [8, 512, 1024], P('ens', None, 'elem'), parts along dimension 0
There are 4 independent parts, one for each index of `ens`. A program takes and returns all parts, laid end to end along the dimension named above; an argument that names none is the same for every part. Nothing has to cross between parts.
Inputs may be any that keep to these rules, and one draw needn't show every extreme that they name: `element_order`: each row is a permutation of the device's slots.
All inputs are finite; a program needn't handle non-finite values.
Results may differ from a plain program's by a relative error of at most 0.0001.
Values sent between devices are 32-bit elements; how exact they have to be, the bound alone decides.
A program may use at most 64 MiB of HBM per device.

v0:
```python
import functools

import jax
import jax.numpy as jnp
import numpy as np
from jax import lax
from jax.experimental import pallas as pl
from jax.experimental.pallas import tpu as pltpu
from jax.sharding import PartitionSpec as P

ORDER = 7
SUBSTEPS = 2
EX = 1
EY = 8
EZ = 16
EXTENT = ORDER + 1
PLANE = EXTENT * EXTENT
NODES = EXTENT * PLANE
MESH = pl.DeviceIdType.MESH


time_step = 0.015


def legendre_table(points, degree):
    table = np.zeros((points.shape[0], degree + 1))
    table[:, 0] = 1.0
    table[:, 1] = points
    for level in range(2, degree + 1):
        table[:, level] = (
            (2 * level - 1) * points * table[:, level - 1] - (level - 1) * table[:, level - 2]
        ) / level
    return table


def gll_derivative(degree):
    extent = degree + 1
    points = np.cos(np.pi * np.arange(extent) / degree)
    for sweep in range(60):
        table = legendre_table(points, degree)
        points = points - (points * table[:, degree] - table[:, degree - 1]) / (
            extent * table[:, degree]
        )
    points = points[::-1].copy()
    values = legendre_table(points, degree)[:, degree]
    matrix = np.zeros((extent, extent))
    for target in range(extent):
        for source in range(extent):
            if target != source:
                matrix[target, source] = values[target] / (
                    values[source] * (points[target] - points[source])
                )
    matrix[0, 0] = -degree * (degree + 1) / 4.0
    matrix[extent - 1, extent - 1] = degree * (degree + 1) / 4.0
    return matrix


def split_matrix():
    derivative = gll_derivative(ORDER).astype(np.float32)
    eye = np.eye(EXTENT, dtype=np.float32)
    full = np.concatenate([np.kron(derivative, eye), np.kron(eye, derivative)], axis=0)
    high = full.astype(jnp.bfloat16)
    low = (full - high.astype(np.float32)).astype(jnp.bfloat16)
    return np.concatenate([high, high, low], axis=1)


def halves(values):
    high = values.astype(jnp.bfloat16)
    low = (values - high.astype(jnp.float32)).astype(jnp.bfloat16)
    return high, low


def lane_forward(values, stride, length):
    total = values.shape[-1]
    near = pltpu.roll(values, total - stride, 1)
    if stride * length == total:
        return near
    coords = lax.broadcasted_iota(jnp.int32, values.shape, 1) // stride % length
    return jnp.where(coords < length - 1, near, pltpu.roll(values, stride * (length - 1), 1))


def lane_backward(values, stride, length):
    total = values.shape[-1]
    near = pltpu.roll(values, stride, 1)
    if stride * length == total:
        return near
    coords = lax.broadcasted_iota(jnp.int32, values.shape, 1) // stride % length
    return jnp.where(coords > 0, near, pltpu.roll(values, total - stride * (length - 1), 1))


def store_assembled(ref, row, values):
    low, high = values[:EXTENT], values[PLANE - EXTENT :]
    ref[row : row + EXTENT] = low + lane_backward(high, EZ, EY)
    ref[row + EXTENT : row + PLANE - EXTENT] = values[EXTENT : PLANE - EXTENT]
    ref[row + PLANE - EXTENT : row + PLANE] = high + lane_forward(low, EZ, EY)
    first = pl.ds(row, EXTENT, stride=EXTENT)
    last = pl.ds(row + ORDER, EXTENT, stride=EXTENT)
    k_low = ref[first, :]
    k_high = ref[last, :]
    ref[first, :] = k_low + lane_backward(k_high, 1, EZ)
    ref[last, :] = k_high + lane_forward(k_low, 1, EZ)


def store_lower(ref, row, values):
    low, high = values[:EXTENT], values[PLANE - EXTENT :]
    ref[row : row + EXTENT] = low + lane_backward(high, EZ, EY)
    ref[row + EXTENT : row + PLANE] = values[EXTENT:]
    first = pl.ds(row, EXTENT, stride=EXTENT)
    k_high = ref[pl.ds(row + ORDER, EXTENT, stride=EXTENT), :]
    ref[first, :] = ref[first, :] + lane_backward(k_high, 1, EZ)


def pack(source, row, target):
    for j in range(ORDER):
        target[j * ORDER : j * ORDER + EXTENT] = source[row + j * EXTENT : row + (j + 1) * EXTENT]


def add_packed(ref, row, packed):
    for j in range(ORDER):
        part = slice(row + j * EXTENT, row + (j + 1) * EXTENT)
        ref[part] = ref[part] + packed[j * ORDER : j * ORDER + EXTENT]
    k_low = ref[pl.ds(row, EXTENT, stride=EXTENT), :]
    ref[pl.ds(row + ORDER, EXTENT, stride=EXTENT), :] = lane_forward(k_low, 1, EZ)
    ref[row + PLANE - EXTENT : row + PLANE] = lane_forward(ref[row : row + EXTENT], EZ, EY)


def kernel(
    count, members, scalars, transport, mass, order, matrix, out,
    speed, current, base, total, work, send, recv, send_sem, recv_sem,
):
    me = lax.axis_index("elem")
    right, left = lax.rem(me + 1, count), lax.rem(me + count - 1, count)
    barrier = pltpu.get_barrier_semaphore()
    for neighbour in (left, right):
        pl.semaphore_signal(barrier, inc=1, device_id={"elem": neighbour}, device_id_type=MESH)

    elements = order.shape[-1]
    lanes = lax.broadcasted_iota(jnp.int32, (elements, elements), 0)
    chosen = jnp.where(order[...] == lanes, 1.0, 0.0).astype(jnp.bfloat16)
    to_brick_matrix = jnp.concatenate([chosen, chosen], axis=1)
    to_slot_matrix = jnp.concatenate([chosen, chosen], axis=0)

    def to_brick(values):
        return lax.dot_general(
            jnp.concatenate(halves(values), axis=1),
            to_brick_matrix,
            (((1,), (1,)), ((), ())),
            preferred_element_type=jnp.float32,
        )

    first_side = 1 - lax.rem(me, 2)
    sides = (first_side, 1 - first_side)

    def copies_of(slot, m):
        copies = []
        for side in sides:
            copies.append(
                pltpu.make_async_remote_copy(
                    src_ref=send.at[slot, m, side, pl.ds(0, ORDER * ORDER)],
                    dst_ref=recv.at[slot, m, side, pl.ds(0, ORDER * ORDER)],
                    send_sem=send_sem.at[slot, m, side],
                    recv_sem=recv_sem.at[slot, m, side],
                    device_id={"elem": side * left + (1 - side) * right},
                    device_id_type=MESH,
                )
            )
        return copies

    def start(slot, m):
        for copy in copies_of(slot, m):
            copy.start()

    def finish(slot, m):
        for copy in copies_of(slot, m):
            copy.wait()

    def row_of(m, i):
        return (m * EXTENT + i) * PLANE

    def rows_of(m, i):
        return slice(row_of(m, i), row_of(m, i) + PLANE)

    def plane_rows(i):
        return slice(i * PLANE, (i + 1) * PLANE)

    def put_face(slot, m, i, value):
        store_lower(work, row_of(m, i), value)
        pack(work, row_of(m, i), send.at[slot, m, 0 if i == ORDER else 1])

    def take_faces(slot, m):
        finish(slot, m)
        add_packed(work, row_of(m, 0), recv.at[slot, m, 0])
        add_packed(work, row_of(m, ORDER), recv.at[slot, m, 1])

    weights = {}
    for i in (0, ORDER):
        weights[i] = to_brick(mass[plane_rows(i), :])
        put_face(1, members, i, weights[i])
    pl.semaphore_wait(barrier, 2)
    start(1, members)
    for m in range(members):
        for i in (0, ORDER):
            put_face(1, m, i, weights[i] * to_brick(scalars[m, plane_rows(i), :]))
        start(1, m)
    for i in range(1, ORDER):
        weight = to_brick(mass[plane_rows(i), :])
        store_assembled(work, row_of(members, i), weight)
        for m in range(members):
            store_assembled(work, row_of(m, i), weight * to_brick(scalars[m, plane_rows(i), :]))
    for r in range(3):
        for i in range(EXTENT):
            speed[r, plane_rows(i), :] = to_brick(transport[r, plane_rows(i), :])

    def begin(m, i):
        value = work[rows_of(m, i), :] * work[rows_of(members, i), :]
        current[0, rows_of(m, i), :] = value
        base[rows_of(m, i), :] = value
        total[rows_of(m, i), :] = value

    def scale(i):
        inverse = 1.0 / work[rows_of(members, i), :]
        work[rows_of(members, i), :] = inverse
        for r in range(3):
            speed[r, plane_rows(i), :] = -speed[r, plane_rows(i), :] * inverse

    for i in range(1, ORDER):
        scale(i)
        for m in range(members):
            begin(m, i)
    take_faces(1, members)
    scale(0)
    scale(ORDER)

    derivative = gll_derivative(ORDER)
    half = EXTENT // 2

    def pair(slot, m, a):
        def plane(i):
            return current[slot, rows_of(m, i), :]

        even = odd = None
        for i in range(half):
            near, far = plane(i), plane(ORDER - i)
            plus = float(derivative[a, i] + derivative[a, ORDER - i]) * 0.5
            minus = float(derivative[a, i] - derivative[a, ORDER - i]) * 0.5
            even_term = plus * (near + far)
            odd_term = minus * (near - far)
            even = even_term if even is None else even + even_term
            odd = odd_term if odd is None else odd + odd_term
        stacked = []
        for i in (a, ORDER - a):
            high, low = halves(plane(i))
            stacked.append(jnp.concatenate([high, low, high], axis=0))
        inside = jnp.dot(
            matrix[...],
            jnp.concatenate(stacked, axis=1),
            preferred_element_type=jnp.float32,
        )
        for place, (i, across) in enumerate(((a, odd + even), (ORDER - a, odd - even))):
            columns = slice(place * elements, (place + 1) * elements)
            yield i, (
                speed[0, plane_rows(i), :] * across
                + speed[1, plane_rows(i), :] * inside[:PLANE, columns]
                + speed[2, plane_rows(i), :] * inside[PLANE:, columns]
            )

    def advance(index, m, i):
        step = lax.rem(index, 4)
        last = step == 3
        weight = jnp.where(jnp.logical_or(step == 0, last), time_step / 6.0, time_step / 3.0)
        reach = jnp.where(step == 2, time_step, 0.5 * time_step)
        tendency = work[rows_of(m, i), :]
        origin = base[rows_of(m, i), :]
        summed = total[rows_of(m, i), :] + weight * tendency
        total[rows_of(m, i), :] = summed
        current[1 - lax.rem(index, 2), rows_of(m, i), :] = jnp.where(
            last, summed, origin + reach * tendency
        )
        base[rows_of(m, i), :] = jnp.where(last, summed, origin)

    def close(index, m):
        take_faces(lax.rem(index, 2), m)
        advance(index, m, 0)
        advance(index, m, ORDER)

    def open_faces(index, m):
        slot = lax.rem(index, 2)
        for i, value in pair(slot, m, 0):
            put_face(slot, m, i, value)
        start(slot, m)

    def interior(index):
        for m in range(members):
            for a in range(1, half):
                for i, value in pair(lax.rem(index, 2), m, a):
                    store_assembled(work, row_of(m, i), value)
                    advance(index, m, i)

    for m in range(members):
        take_faces(1, m)
        begin(m, 0)
        begin(m, ORDER)
        open_faces(0, m)
    interior(0)

    def stage(index, carry):
        for m in range(members):
            close(index - 1, m)
            open_faces(index, m)
        interior(index)
        return carry

    final = 4 * SUBSTEPS - 1
    lax.fori_loop(1, final + 1, stage, 0)
    for m in range(members):
        close(final, m)
        out[m, :, :] = jnp.dot(
            jnp.concatenate(halves(total[m * NODES : (m + 1) * NODES, :]), axis=1),
            to_slot_matrix,
            preferred_element_type=jnp.float32,
        )


def per_device(scalars, transport, mass, element_order):
    members, nodes, elements = scalars.shape
    count = lax.axis_size("elem")
    whole = pl.BlockSpec(memory_space=pltpu.VMEM)
    return pl.pallas_call(
        functools.partial(kernel, count, members),
        out_shape=jax.ShapeDtypeStruct(scalars.shape, jnp.float32),
        in_specs=[whole] * 5,
        out_specs=whole,
        scratch_shapes=[
            pltpu.VMEM((3, nodes, elements), jnp.float32),
            pltpu.VMEM((2, members * nodes, elements), jnp.float32),
            pltpu.VMEM((members * nodes, elements), jnp.float32),
            pltpu.VMEM((members * nodes, elements), jnp.float32),
            pltpu.VMEM(((members + 1) * nodes, elements), jnp.float32),
            pltpu.VMEM((2, members + 1, 2, PLANE - EXTENT, elements), jnp.float32),
            pltpu.VMEM((2, members + 1, 2, PLANE - EXTENT, elements), jnp.float32),
            pltpu.SemaphoreType.DMA((2, members + 1, 2)),
            pltpu.SemaphoreType.DMA((2, members + 1, 2)),
        ],
        compiler_params=pltpu.CompilerParams(collective_id=0, has_side_effects=True),
    )(scalars, transport, mass, element_order, jnp.asarray(split_matrix()))


def solution(mesh):
    in_specs = (P("ens", None, "elem"), P(None, None, "elem"), P(None, "elem"), P("elem", None))
    out_specs = P("ens", None, "elem")
    return jax.shard_map(
        per_device, mesh=mesh, in_specs=in_specs, out_specs=out_specs, check_vma=False
    )
```

profile of v0, /device:TPU:0, one launch (start us, length us, event | category | flops | bytes accessed | tf_op | source)
XLA Modules:
  0.0 51.4 jit_solution(13335275091358603803)
XLA Ops:
  0.0 49.5 %shard_map.55 = f32[2,512,128]{2,1,0:T(8,128)} custom-call(f32[2,512,128]{2,1,0:T(8,128)} %scalars.1, f32[3,512,128]{2,1,0:T(8,128)} %transport.1, f32[512,128]{1,0:T(8,128)} %mass.1, s32[1,128]{1,0:T(1,128)} %order.1, bf16[128,192]{1,0:T(8,128)(2,1)} %constant.2.clone.matrix), custom_call_target="tpu_custom_call" | custom-call | tf_op jit(solution)/shard_map/pallas_call | solution.py:328
  49.5 1.9 %copy.7 = f32[2,512,128]{2,1,0:T(8,128)} copy(f32[2,512,128]{2,1,0:T(8,128)} %shard_map.55) | data formatting | bytes 1048576
where the time goes:
time: 51.6 us; the launch traced here: 51.4 us
  Pallas kernels  49.5 us (96%)
  local copies, waits for them, and re-layouts  1.87 us (4%)
    pallas_call x1, Pallas kernels, per_device(): pl.pallas_call(functools.partial(kernel, count, members), out_shape=jax.S...  49.5 us
    unnamed x1, local copies, waits for them, and re-layouts  1.87 us

commit v1 on v0

v1 whole, which is shorter than its diff:
```python
import functools

import jax
import jax.numpy as jnp
import numpy as np
from jax import lax
from jax.experimental import pallas as pl
from jax.experimental.pallas import tpu as pltpu
from jax.sharding import PartitionSpec as P

ORDER = 7
SUBSTEPS = 2
EX = 1
EY = 8
EZ = 16
EXTENT = ORDER + 1
PLANE = EXTENT * EXTENT
NODES = EXTENT * PLANE
MESH = pl.DeviceIdType.MESH
NEAR, FAR, NEXT = 0, 1, 2


time_step = 0.015


def legendre_table(points, degree):
    table = np.zeros((points.shape[0], degree + 1))
    table[:, 0] = 1.0
    table[:, 1] = points
    for level in range(2, degree + 1):
        table[:, level] = (
            (2 * level - 1) * points * table[:, level - 1] - (level - 1) * table[:, level - 2]
        ) / level
    return table


def gll_derivative(degree):
    extent = degree + 1
    points = np.cos(np.pi * np.arange(extent) / degree)
    for sweep in range(60):
        table = legendre_table(points, degree)
        points = points - (points * table[:, degree] - table[:, degree - 1]) / (
            extent * table[:, degree]
        )
    points = points[::-1].copy()
    values = legendre_table(points, degree)[:, degree]
    matrix = np.zeros((extent, extent))
    for target in range(extent):
        for source in range(extent):
            if target != source:
                matrix[target, source] = values[target] / (
                    values[source] * (points[target] - points[source])
                )
    matrix[0, 0] = -degree * (degree + 1) / 4.0
    matrix[extent - 1, extent - 1] = degree * (degree + 1) / 4.0
    return matrix


def split_matrix():
    derivative = gll_derivative(ORDER).astype(np.float32)
    eye = np.eye(EXTENT, dtype=np.float32)
    full = np.concatenate([np.kron(derivative, eye), np.kron(eye, derivative)], axis=0)
    high = full.astype(jnp.bfloat16)
    low = (full - high.astype(np.float32)).astype(jnp.bfloat16)
    return np.concatenate([high, high, low], axis=1)


def halves(values):
    high = values.astype(jnp.bfloat16)
    low = (values - high.astype(jnp.float32)).astype(jnp.bfloat16)
    return high, low


def lane_forward(values, stride, length):
    total = values.shape[-1]
    near = pltpu.roll(values, total - stride, 1)
    if stride * length == total:
        return near
    coords = lax.broadcasted_iota(jnp.int32, values.shape, 1) // stride % length
    return jnp.where(coords < length - 1, near, pltpu.roll(values, stride * (length - 1), 1))


def lane_backward(values, stride, length):
    total = values.shape[-1]
    near = pltpu.roll(values, stride, 1)
    if stride * length == total:
        return near
    coords = lax.broadcasted_iota(jnp.int32, values.shape, 1) // stride % length
    return jnp.where(coords > 0, near, pltpu.roll(values, total - stride * (length - 1), 1))


def store_assembled(ref, row, values):
    low, high = values[:EXTENT], values[PLANE - EXTENT :]
    ref[row : row + EXTENT] = low + lane_backward(high, EZ, EY)
    ref[row + EXTENT : row + PLANE - EXTENT] = values[EXTENT : PLANE - EXTENT]
    ref[row + PLANE - EXTENT : row + PLANE] = high + lane_forward(low, EZ, EY)
    first = pl.ds(row, EXTENT, stride=EXTENT)
    last = pl.ds(row + ORDER, EXTENT, stride=EXTENT)
    k_low = ref[first, :]
    k_high = ref[last, :]
    ref[first, :] = k_low + lane_backward(k_high, 1, EZ)
    ref[last, :] = k_high + lane_forward(k_low, 1, EZ)


def store_lower(ref, row, values):
    low, high = values[:EXTENT], values[PLANE - EXTENT :]
    ref[row : row + EXTENT] = low + lane_backward(high, EZ, EY)
    ref[row + EXTENT : row + PLANE] = values[EXTENT:]
    first = pl.ds(row, EXTENT, stride=EXTENT)
    k_high = ref[pl.ds(row + ORDER, EXTENT, stride=EXTENT), :]
    ref[first, :] = ref[first, :] + lane_backward(k_high, 1, EZ)


def pack(source, row, target):
    for j in range(ORDER):
        target[j * ORDER : j * ORDER + EXTENT] = source[row + j * EXTENT : row + (j + 1) * EXTENT]


def add_packed(ref, row, packed):
    for j in range(ORDER):
        part = slice(row + j * EXTENT, row + (j + 1) * EXTENT)
        ref[part] = ref[part] + packed[j * ORDER : j * ORDER + EXTENT]
    k_low = ref[pl.ds(row, EXTENT, stride=EXTENT), :]
    ref[pl.ds(row + ORDER, EXTENT, stride=EXTENT), :] = lane_forward(k_low, 1, EZ)
    ref[row + PLANE - EXTENT : row + PLANE] = lane_forward(ref[row : row + EXTENT], EZ, EY)


def expand_packed(ref, row, packed, scale):
    for j in range(ORDER):
        ref[row + j * EXTENT : row + (j + 1) * EXTENT] = (
            scale * packed[j * ORDER : j * ORDER + EXTENT]
        )
    spread_lower(ref, row)


def spread_lower(ref, row):
    k_low = ref[pl.ds(row, EXTENT, stride=EXTENT), :]
    ref[pl.ds(row + ORDER, EXTENT, stride=EXTENT), :] = lane_forward(k_low, 1, EZ)
    ref[row + PLANE - EXTENT : row + PLANE] = lane_forward(ref[row : row + EXTENT], EZ, EY)


def kernel(
    count, members, scalars, transport, mass, order, matrix, state,
    speed, middle, ahead, work, raw, near, far, joint, cross, beyond,
    mass_send, mass_recv, mass_send_sem, mass_recv_sem,
    coef_send, coef_recv, coef_send_sem, coef_recv_sem,
    send, recv, send_sem, recv_sem,
):
    me = lax.axis_index("elem")

    def shifted(distance):
        return lax.rem(me + distance + count, count)

    barrier = pltpu.get_barrier_semaphore()
    for distance in (-2, -1, 1, 2):
        pl.semaphore_signal(
            barrier, inc=1, device_id={"elem": shifted(distance)}, device_id_type=MESH
        )

    elements = order.shape[-1]
    lanes = lax.broadcasted_iota(jnp.int32, (elements, elements), 0)
    chosen = jnp.where(order[...] == lanes, 1.0, 0.0).astype(jnp.bfloat16)
    to_brick_matrix = jnp.concatenate([chosen, chosen], axis=1)

    def to_brick(values):
        return lax.dot_general(
            jnp.concatenate(halves(values), axis=1),
            to_brick_matrix,
            (((1,), (1,)), ((), ())),
            preferred_element_type=jnp.float32,
        )

    first_side = 1 - lax.rem(me, 2)
    sides = (first_side, 1 - first_side)
    ends = (ORDER, 0)

    def target(side, distance):
        return {"elem": lax.rem(me + count + distance * (1 - 2 * side), count)}

    def mass_copies(m):
        return [
            pltpu.make_async_remote_copy(
                src_ref=mass_send.at[m, side, pl.ds(0, ORDER * ORDER)],
                dst_ref=mass_recv.at[m, side, pl.ds(0, ORDER * ORDER)],
                send_sem=mass_send_sem.at[m, side],
                recv_sem=mass_recv_sem.at[m, side],
                device_id=target(side, 1),
                device_id_type=MESH,
            )
            for side in sides
        ]

    def coef_copies():
        return [
            pltpu.make_async_remote_copy(
                src_ref=coef_send.at[side],
                dst_ref=coef_recv.at[side],
                send_sem=coef_send_sem.at[side],
                recv_sem=coef_recv_sem.at[side],
                device_id=target(side, 1),
                device_id_type=MESH,
            )
            for side in sides
        ]

    def face_copies(slot, m, kinds):
        return [
            pltpu.make_async_remote_copy(
                src_ref=send.at[slot, m, side, kind // 2, pl.ds(0, ORDER * ORDER)],
                dst_ref=recv.at[slot, m, side, kind, pl.ds(0, ORDER * ORDER)],
                send_sem=send_sem.at[slot, m, side, kind],
                recv_sem=recv_sem.at[slot, m, side, kind],
                device_id=target(side, 2 if kind == FAR else 1),
                device_id_type=MESH,
            )
            for side in sides
            for kind in kinds
        ]

    def row_of(m, i):
        return (m * EXTENT + i) * PLANE

    def rows_of(m, i):
        return slice(row_of(m, i), row_of(m, i) + PLANE)

    def plane_rows(i):
        return slice(i * PLANE, (i + 1) * PLANE)

    def block(values, place):
        return values[place * PLANE : (place + 1) * PLANE]

    def side_rows(m, side):
        return slice((m * 2 + side) * PLANE, (m * 2 + side + 1) * PLANE)

    outer = to_brick(
        jnp.concatenate(
            [mass[plane_rows(i), :] for i in ends]
            + [scalars[m, plane_rows(i), :] for m in range(members) for i in ends],
            axis=0,
        )
    )
    for side, i in enumerate(ends):
        store_lower(work, row_of(members, i), block(outer, side))
        pack(work, row_of(members, i), mass_send.at[members, side])
    for m in range(members):
        for side, i in enumerate(ends):
            store_lower(
                work, row_of(m, i), block(outer, side) * block(outer, 2 * (m + 1) + side)
            )
            pack(work, row_of(m, i), mass_send.at[m, side])
    pl.semaphore_wait(barrier, 4)
    for m in (members, *range(members)):
        for copy in mass_copies(m):
            copy.start()

    outer = to_brick(
        jnp.concatenate([transport[r, plane_rows(i), :] for r in range(3) for i in ends], axis=0)
    )
    for r in range(3):
        for side, i in enumerate(ends):
            speed[r, plane_rows(i), :] = block(outer, 2 * r + side)
            coef_send[side, r] = block(outer, 2 * r + side)
    for copy in coef_copies():
        copy.start()

    inner = slice(PLANE, NODES - PLANE)
    for r in range(3):
        speed[r, inner, :] = to_brick(transport[r, inner, :])
    middle[inner, :] = to_brick(mass[inner, :])
    for m in range(members):
        rows = slice(m * NODES + PLANE, (m + 1) * NODES - PLANE)
        ahead[rows, :] = to_brick(scalars[m, inner, :])
    for i in range(1, ORDER):
        weight = middle[plane_rows(i), :]
        store_assembled(work, row_of(members, i), weight)
        for m in range(members):
            store_assembled(work, row_of(m, i), weight * ahead[rows_of(m, i), :])

    def begin(m, i):
        state[0, rows_of(m, i), :] = work[rows_of(m, i), :] * work[rows_of(members, i), :]

    def scale(i):
        inverse = 1.0 / work[rows_of(members, i), :]
        work[rows_of(members, i), :] = inverse
        for r in range(3):
            speed[r, plane_rows(i), :] = speed[r, plane_rows(i), :] * (-time_step * inverse)

    for i in range(1, ORDER):
        scale(i)
        for m in range(members):
            begin(m, i)

    def take_masses(m):
        for copy in mass_copies(m):
            copy.wait()
        add_packed(work, row_of(m, 0), mass_recv.at[m, 0])
        add_packed(work, row_of(m, ORDER), mass_recv.at[m, 1])

    take_masses(members)
    scale(0)
    scale(ORDER)

    derivative = gll_derivative(ORDER)
    half = EXTENT // 2

    def inside_of(planes):
        stacked = []
        for values in planes:
            high, low = halves(values)
            stacked.append(jnp.concatenate([high, low, high], axis=0))
        return jnp.dot(
            matrix[...], jnp.concatenate(stacked, axis=1), preferred_element_type=jnp.float32
        )

    def pair(plane, a):
        even = odd = None
        for i in range(half):
            one, other = plane(i), plane(ORDER - i)
            plus = float(derivative[a, i] + derivative[a, ORDER - i]) * 0.5
            minus = float(derivative[a, i] - derivative[a, ORDER - i]) * 0.5
            even_term = plus * (one + other)
            odd_term = minus * (one - other)
            even = even_term if even is None else even + even_term
            odd = odd_term if odd is None else odd + odd_term
        inside = inside_of([plane(a), plane(ORDER - a)])
        for place, (i, across) in enumerate(((a, odd + even), (ORDER - a, odd - even))):
            columns = slice(place * elements, (place + 1) * elements)
            yield i, (
                speed[0, plane_rows(i), :] * across
                + speed[1, plane_rows(i), :] * inside[:PLANE, columns]
                + speed[2, plane_rows(i), :] * inside[PLANE:, columns]
            )

    def reaches(slot):
        return jnp.where(slot == 0, 0.25, 0.5), jnp.where(slot == 0, 1.0 / 3.0, 1.0)

    def first_faces(index, m):
        slot = lax.rem(index, 2)
        for i, value in pair(lambda n: state[slot, rows_of(m, n), :], 0):
            side = ends.index(i)
            store_lower(work, row_of(m, i), value)
            pack(work, row_of(m, i), send.at[slot, m, side, 0])
        for copy in face_copies(slot, m, (FAR, NEAR)):
            copy.start()

    def first_inner(index, m):
        slot = lax.rem(index, 2)
        reach, _ = reaches(slot)
        for i in ends:
            spread_lower(work, row_of(m, i))
            middle[rows_of(m, i), :] = state[0, rows_of(m, i), :] + reach * work[rows_of(m, i), :]
        for a in range(1, half):
            for i, value in pair(lambda n: state[slot, rows_of(m, n), :], a):
                store_assembled(work, row_of(m, i), value)
                middle[rows_of(m, i), :] = (
                    state[0, rows_of(m, i), :] + reach * work[rows_of(m, i), :]
                )
        for side, i in enumerate(ends):
            across = None
            for n in range(EXTENT):
                if n != i:
                    term = float(derivative[i, n]) * middle[rows_of(m, n), :]
                    across = term if across is None else across + term
            value = speed[0, plane_rows(i), :] * across
            raw[side_rows(m, side), :] = value
            store_lower(work, row_of(m, i), value)
            pack(work, row_of(m, i), send.at[slot, m, side, 1])
        for copy in face_copies(slot, m, (NEXT,)):
            copy.start()

    def second_ahead(index, m):
        _, reach = reaches(lax.rem(index, 2))
        for a in range(1, half):
            for i, value in pair(lambda n: middle[rows_of(m, n), :], a):
                store_assembled(work, row_of(m, i), value)
                ahead[rows_of(m, i), :] = (
                    state[0, rows_of(m, i), :] + reach * work[rows_of(m, i), :]
                )

    def second(index, m):
        slot = lax.rem(index, 2)
        reach, final_reach = reaches(slot)
        for copy in face_copies(slot, m, (NEAR, FAR, NEXT)):
            copy.wait()
        planes = (0, ORDER)
        for side, i in enumerate(planes):
            row = (m * 2 + side) * PLANE
            expand_packed(near, row, recv.at[slot, m, side, NEAR], reach)
            expand_packed(far, row, recv.at[slot, m, side, FAR], reach)
        deltas = [near[side_rows(m, side), :] for side in range(2)]
        faces = [middle[rows_of(m, i), :] + deltas[side] for side, i in enumerate(planes)]
        inside = inside_of(faces)
        for side, i in enumerate(planes):
            columns = slice(side * elements, (side + 1) * elements)
            value = (
                joint[side, 0] * faces[side]
                + joint[side, 1] * inside[:PLANE, columns]
                + joint[side, 2] * inside[PLANE:, columns]
                + cross[side] * deltas[1 - side]
                + beyond[side] * far[side_rows(m, side), :]
                + raw[side_rows(m, 1 - side), :]
            )
            store_lower(work, row_of(m, i), value)
            add_packed(work, row_of(m, i), recv.at[slot, m, side, NEXT])
        for i in planes:
            state[1 - slot, rows_of(m, i), :] = (
                state[0, rows_of(m, i), :] + final_reach * work[rows_of(m, i), :]
            )
        low, high = (final_reach * delta for delta in deltas)
        for i in range(1, ORDER):
            across = float(derivative[i, 0]) * low + float(derivative[i, ORDER]) * high
            store_assembled(work, row_of(m, i), speed[0, plane_rows(i), :] * across)
            state[1 - slot, rows_of(m, i), :] = ahead[rows_of(m, i), :] + work[rows_of(m, i), :]

    for m in range(members):
        take_masses(m)
        begin(m, 0)
        begin(m, ORDER)
        first_faces(0, m)
        first_inner(0, m)

    for copy in coef_copies():
        copy.wait()
    for side, i in enumerate((0, ORDER)):
        inverse = -time_step * work[rows_of(members, i), :]
        theirs = coef_recv[side, 0] * inverse
        ours = speed[0, plane_rows(i), :]
        joint[side, 0] = float(derivative[i, i]) * ours + (
            float(derivative[ORDER - i, ORDER - i]) * theirs
        )
        cross[side] = float(derivative[i, ORDER - i]) * ours
        beyond[side] = float(derivative[ORDER - i, i]) * theirs
        for r in (1, 2):
            joint[side, r] = speed[r, plane_rows(i), :] + coef_recv[side, r] * inverse
    for m in range(members):
        second_ahead(0, m)

    def stage(index, carry):
        for m in range(members):
            second(index - 1, m)
            first_faces(index, m)
            first_inner(index, m)
        for m in range(members):
            second_ahead(index, m)
        return carry

    final = 2 * SUBSTEPS - 1
    lax.fori_loop(1, final + 1, stage, 0)
    for m in range(members):
        second(final, m)


def slot_kernel(members, order, state, out):
    elements = order.shape[-1]
    lanes = lax.broadcasted_iota(jnp.int32, (elements, elements), 0)
    chosen = jnp.where(order[...] == lanes, 1.0, 0.0).astype(jnp.bfloat16)
    to_slot_matrix = jnp.concatenate([chosen, chosen], axis=0)
    for m in range(members):
        out[m, :, :] = jnp.dot(
            jnp.concatenate(halves(state[0, m * NODES : (m + 1) * NODES, :]), axis=1),
            to_slot_matrix,
            preferred_element_type=jnp.float32,
        )


def per_device(scalars, transport, mass, element_order):
    members, nodes, elements = scalars.shape
    count = lax.axis_size("elem")
    whole = pl.BlockSpec(memory_space=pltpu.VMEM)

    def floats(*shape):
        return pltpu.VMEM((*shape, elements), jnp.float32)

    def semaphores(*shape):
        return pltpu.SemaphoreType.DMA(shape)

    state = pl.pallas_call(
        functools.partial(kernel, count, members),
        out_shape=floats(2, members * nodes),
        in_specs=[whole] * 5,
        out_specs=whole,
        scratch_shapes=[
            floats(3, nodes),
            floats(members * nodes),
            floats(members * nodes),
            floats((members + 1) * nodes),
            floats(members * 2 * PLANE),
            floats(members * 2 * PLANE),
            floats(members * 2 * PLANE),
            floats(2, 3, PLANE),
            floats(2, PLANE),
            floats(2, PLANE),
            floats(members + 1, 2, PLANE - EXTENT),
            floats(members + 1, 2, PLANE - EXTENT),
            semaphores(members + 1, 2),
            semaphores(members + 1, 2),
            floats(2, 3, PLANE),
            floats(2, 3, PLANE),
            semaphores(2),
            semaphores(2),
            floats(2, members, 2, 2, PLANE - EXTENT),
            floats(2, members, 2, 3, PLANE - EXTENT),
            semaphores(2, members, 2, 3),
            semaphores(2, members, 2, 3),
        ],
        compiler_params=pltpu.CompilerParams(collective_id=0, has_side_effects=True),
    )(scalars, transport, mass, element_order, jnp.asarray(split_matrix()))
    return pl.pallas_call(
        functools.partial(slot_kernel, members),
        out_shape=jax.ShapeDtypeStruct(scalars.shape, jnp.float32),
        in_specs=[whole] * 2,
        out_specs=whole,
    )(element_order, pltpu.with_memory_space_constraint(state, pltpu.VMEM))


def solution(mesh):
    in_specs = (P("ens", None, "elem"), P(None, None, "elem"), P(None, "elem"), P("elem", None))
    out_specs = P("ens", None, "elem")
    return jax.shard_map(
        per_device, mesh=mesh, in_specs=in_specs, out_specs=out_specs, check_vma=False
    )
```

time: 51.6 us -> 43.8 us (0.85)
  Pallas kernels: 49.5 us -> 43.6 us
  local copies, waits for them, and re-layouts: 1.87 us -> 0 us
    pallas_call x1 -> x2, Pallas kernels: 49.5 us -> 43.6 us  [the longest x1 41.9 us: per_device(): pl.pallas_call(functools.partial(kernel, count, members), out_shape=float...]
    unnamed x1 -> x0, local copies, waits for them, and re-layouts: 1.87 us -> none
where the time goes in v1:
time: 43.8 us; the launch traced here: 43.7 us
  Pallas kernels  43.6 us (100%)
    pallas_call x1, Pallas kernels, per_device(): pl.pallas_call(functools.partial(kernel, count, members), out_shape=float...  41.9 us
    pallas_call x1, Pallas kernels, per_device(): pl.pallas_call(functools.partial(slot_kernel, members), out_shape=jax.Sha...  1.76 us

profile of v1, /device:TPU:0, one launch (start us, length us, event | category | flops | bytes accessed | tf_op | source)
XLA Modules:
  0.0 43.7 jit_solution(12968103302421091411)
XLA Ops:
  0.0 41.9 %shard_map.55.state = f32[2,1024,128]{2,1,0:T(8,128)S(1)} custom-call(f32[2,512,128]{2,1,0:T(8,128)} %scalars.1, f32[3,512,128]{2,1,0:T(8,128)} %transport.1, f32[512,128]{1,0:T(8,128)} %mass.1, s32[1,128]{1,0:T(1,128)} %order.3, bf16[128,192]{1,0:T(8,128)(2,1)} %constant.2.clone.matrix), custom_call_target="tpu_custom_call" | custom-call | tf_op jit(solution)/shard_map/pallas_call | solution.py:477
  41.9 1.8 %shard_map.56 = f32[2,512,128]{2,1,0:T(8,128)} custom-call(s32[1,128]{1,0:T(1,128)} %order.3, f32[2,1024,128]{2,1,0:T(8,128)S(1)} %shard_map.55.state), custom_call_target="tpu_custom_call" | custom-call | tf_op jit(solution)/shard_map/pallas_call | solution.py:508

commit v2 on v1

--- a/solution.py
+++ b/solution.py
@@ -140,22 +140,40 @@
 
 
 def kernel(
-    count, members, scalars, transport, mass, order, matrix, state,
-    speed, middle, ahead, work, raw, near, far, joint, cross, beyond,
+    count, members, groups, scalars_in, transport_in, mass_in, order_in, matrix_in, out,
+    state,    scalars, transport, mass, order, matrix, load_sem, speed, middle, ahead, work, raw, near, far, joint, cross, beyond,
     mass_send, mass_recv, mass_send_sem, mass_recv_sem,
-    coef_send, coef_recv, coef_send_sem, coef_recv_sem,
+    coef_send, coef_recv, coef_send_sem, coef_recv_sem, share_send_sem, share_recv_sem,
     send, recv, send_sem, recv_sem,
 ):
-    me = lax.axis_index("elem")
+    me, group = lax.axis_index("elem"), lax.axis_index("ens")
 
     def shifted(distance):
         return lax.rem(me + distance + count, count)
+
+    def peer(distance):
+        return {"ens": lax.rem(group + distance, groups)}
 
     barrier = pltpu.get_barrier_semaphore()
     for distance in (-2, -1, 1, 2):
         pl.semaphore_signal(
             barrier, inc=1, device_id={"elem": shifted(distance)}, device_id_type=MESH
         )
+    for distance in range(1, groups):
+        pl.semaphore_signal(barrier, inc=1, device_id=peer(distance), device_id_type=MESH)
+
+    loads = [
+        pltpu.make_async_copy(source, place, load_sem.at[number])
+        for number, (source, place) in enumerate(
+            (
+                (order_in, order), (mass_in, mass), (scalars_in, scalars),
+                (transport_in, transport), (matrix_in, matrix),
+            )
+        )
+    ]
+    for load in loads:
+        load.start()
+    loads[0].wait()
 
     elements = order.shape[-1]
     lanes = lax.broadcasted_iota(jnp.int32, (elements, elements), 0)
@@ -190,16 +208,33 @@
             for side in sides
         ]
 
+    share = 3 * PLANE // groups
+    shared = pl.ds(pl.multiple_of(group * share, 8), share)
+
     def coef_copies():
         return [
             pltpu.make_async_remote_copy(
-                src_ref=coef_send.at[side],
-                dst_ref=coef_recv.at[side],
+                src_ref=coef_send.at[side, shared],
+                dst_ref=coef_recv.at[side, shared],
                 send_sem=coef_send_sem.at[side],
                 recv_sem=coef_recv_sem.at[side],
                 device_id=target(side, 1),
                 device_id_type=MESH,
             )
+            for side in sides
+        ]
+
+    def share_copies():
+        return [
+            pltpu.make_async_remote_copy(
+                src_ref=coef_recv.at[side, shared],
+                dst_ref=coef_recv.at[side, shared],
+                send_sem=share_send_sem.at[distance - 1, side],
+                recv_sem=share_recv_sem.at[distance - 1, side],
+                device_id=peer(distance),
+                device_id_type=MESH,
+            )
+            for distance in range(1, groups)
             for side in sides
         ]
 
@@ -232,6 +267,8 @@
     def side_rows(m, side):
         return slice((m * 2 + side) * PLANE, (m * 2 + side + 1) * PLANE)
 
+    loads[1].wait()
+    loads[2].wait()
     outer = to_brick(
         jnp.concatenate(
             [mass[plane_rows(i), :] for i in ends]
@@ -248,18 +285,20 @@
                 work, row_of(m, i), block(outer, side) * block(outer, 2 * (m + 1) + side)
             )
             pack(work, row_of(m, i), mass_send.at[m, side])
-    pl.semaphore_wait(barrier, 4)
+    pl.semaphore_wait(barrier, 4 + groups - 1)
     for m in (members, *range(members)):
         for copy in mass_copies(m):
             copy.start()
 
+    loads[3].wait()
+    loads[4].wait()
     outer = to_brick(
         jnp.concatenate([transport[r, plane_rows(i), :] for r in range(3) for i in ends], axis=0)
     )
     for r in range(3):
         for side, i in enumerate(ends):
             speed[r, plane_rows(i), :] = block(outer, 2 * r + side)
-            coef_send[side, r] = block(outer, 2 * r + side)
+            coef_send[side, plane_rows(r), :] = block(outer, 2 * r + side)
     for copy in coef_copies():
         copy.start()
 
@@ -421,9 +460,13 @@
 
     for copy in coef_copies():
         copy.wait()
+    for copy in share_copies():
+        copy.start()
+    for copy in share_copies():
+        copy.wait()
     for side, i in enumerate((0, ORDER)):
         inverse = -time_step * work[rows_of(members, i), :]
-        theirs = coef_recv[side, 0] * inverse
+        theirs = coef_recv[side, plane_rows(0), :] * inverse
         ours = speed[0, plane_rows(i), :]
         joint[side, 0] = float(derivative[i, i]) * ours + (
             float(derivative[ORDER - i, ORDER - i]) * theirs
@@ -431,7 +474,7 @@
         cross[side] = float(derivative[i, ORDER - i]) * ours
         beyond[side] = float(derivative[ORDER - i, i]) * theirs
         for r in (1, 2):
-            joint[side, r] = speed[r, plane_rows(i), :] + coef_recv[side, r] * inverse
+            joint[side, r] = speed[r, plane_rows(i), :] + coef_recv[side, plane_rows(r), :] * inverse
     for m in range(members):
         second_ahead(0, m)
 
@@ -448,25 +491,24 @@
     lax.fori_loop(1, final + 1, stage, 0)
     for m in range(members):
         second(final, m)
-
-
-def slot_kernel(members, order, state, out):
-    elements = order.shape[-1]
-    lanes = lax.broadcasted_iota(jnp.int32, (elements, elements), 0)
-    chosen = jnp.where(order[...] == lanes, 1.0, 0.0).astype(jnp.bfloat16)
-    to_slot_matrix = jnp.concatenate([chosen, chosen], axis=0)
-    for m in range(members):
         out[m, :, :] = jnp.dot(
             jnp.concatenate(halves(state[0, m * NODES : (m + 1) * NODES, :]), axis=1),
-            to_slot_matrix,
+            jnp.concatenate([chosen, chosen], axis=0),
             preferred_element_type=jnp.float32,
         )
+
+
+def store_kernel(result, out, store_sem):
+    copy = pltpu.make_async_copy(result, out, store_sem)
+    copy.start()
+    copy.wait()
 
 
 def per_device(scalars, transport, mass, element_order):
     members, nodes, elements = scalars.shape
-    count = lax.axis_size("elem")
+    count, groups = lax.axis_size("elem"), lax.axis_size("ens")
     whole = pl.BlockSpec(memory_space=pltpu.VMEM)
+    matrix = jnp.asarray(split_matrix())
 
     def floats(*shape):
         return pltpu.VMEM((*shape, elements), jnp.float32)
@@ -474,12 +516,19 @@
     def semaphores(*shape):
         return pltpu.SemaphoreType.DMA(shape)
 
-    state = pl.pallas_call(
-        functools.partial(kernel, count, members),
-        out_shape=floats(2, members * nodes),
-        in_specs=[whole] * 5,
+    result = pl.pallas_call(
+        functools.partial(kernel, count, members, groups),
+        out_shape=floats(members, nodes),
+        in_specs=[pl.BlockSpec(memory_space=pl.ANY)] * 5,
         out_specs=whole,
         scratch_shapes=[
+            floats(2, members * nodes),
+            floats(members, nodes),
+            floats(3, nodes),
+            floats(nodes),
+            pltpu.VMEM(element_order.shape, jnp.int32),
+            pltpu.VMEM(matrix.shape, matrix.dtype),
+            semaphores(5),
             floats(3, nodes),
             floats(members * nodes),
             floats(members * nodes),
@@ -494,23 +543,26 @@
             floats(members + 1, 2, PLANE - EXTENT),
             semaphores(members + 1, 2),
             semaphores(members + 1, 2),
-            floats(2, 3, PLANE),
-            floats(2, 3, PLANE),
+            floats(2, 3 * PLANE),
+            floats(2, 3 * PLANE),
             semaphores(2),
             semaphores(2),
+            semaphores(groups - 1, 2),
+            semaphores(groups - 1, 2),
             floats(2, members, 2, 2, PLANE - EXTENT),
             floats(2, members, 2, 3, PLANE - EXTENT),
             semaphores(2, members, 2, 3),
             semaphores(2, members, 2, 3),
         ],
         compiler_params=pltpu.CompilerParams(collective_id=0, has_side_effects=True),
-    )(scalars, transport, mass, element_order, jnp.asarray(split_matrix()))
+    )(scalars, transport, mass, element_order, matrix)
     return pl.pallas_call(
-        functools.partial(slot_kernel, members),
+        store_kernel,
         out_shape=jax.ShapeDtypeStruct(scalars.shape, jnp.float32),
-        in_specs=[whole] * 2,
-        out_specs=whole,
-    )(element_order, pltpu.with_memory_space_constraint(state, pltpu.VMEM))
+        in_specs=[whole],
+        out_specs=pl.BlockSpec(memory_space=pl.ANY),
+        scratch_shapes=[pltpu.SemaphoreType.DMA],
+    )(pltpu.with_memory_space_constraint(result, pltpu.VMEM))
 
 
 def solution(mesh):

time: 43.8 us -> 40.9 us (0.934)
  Pallas kernels: 43.6 us -> 40.7 us
    pallas_call x2, Pallas kernels: 43.6 us -> 40.7 us  [the longest x1 39.9 us: per_device(): pl.pallas_call(functools.partial(kernel, count, members, groups), out_sha...]
where the time goes in v2:
time: 40.9 us; the launch traced here: 40.7 us
  Pallas kernels  40.7 us (100%)
    pallas_call x1, Pallas kernels, per_device(): pl.pallas_call(functools.partial(kernel, count, members, groups), out_sha...  39.9 us

profile of v2, /device:TPU:0, one launch (start us, length us, event | category | flops | bytes accessed | tf_op | source)
XLA Modules:
  0.0 40.7 jit_solution(12950847163750205432)
XLA Ops:
  0.0 39.9 %shard_map.55.result = f32[2,512,128]{2,1,0:T(8,128)S(1)} custom-call(f32[2,512,128]{2,1,0:T(8,128)} %scalars_in.1, f32[3,512,128]{2,1,0:T(8,128)} %transport_in.1, f32[512,128]{1,0:T(8,128)} %mass_in.1, s32[1,128]{1,0:T(1,128)} %order_in.1, bf16[128,192]{1,0:T(8,128)(2,1)} %constant.2.clone.matrix_in), custom_call_target="tpu_custom_call" | custom-call | tf_op jit(solution)/shard_map/pallas_call | solution.py:519
  39.9 0.8 %shard_map.56 = f32[2,512,128]{2,1,0:T(8,128)} custom-call(f32[2,512,128]{2,1,0:T(8,128)S(1)} %shard_map.55.result), custom_call_target="tpu_custom_call" | custom-call | tf_op jit(solution)/shard_map/pallas_call | solution.py:559

commit v3 on v2

--- a/solution.py
+++ b/solution.py
@@ -102,46 +102,98 @@
     ref[last, :] = k_high + lane_forward(k_low, 1, EZ)
 
 
-def store_lower(ref, row, values):
-    low, high = values[:EXTENT], values[PLANE - EXTENT :]
-    ref[row : row + EXTENT] = low + lane_backward(high, EZ, EY)
-    ref[row + EXTENT : row + PLANE] = values[EXTENT:]
-    first = pl.ds(row, EXTENT, stride=EXTENT)
-    k_high = ref[pl.ds(row + ORDER, EXTENT, stride=EXTENT), :]
-    ref[first, :] = ref[first, :] + lane_backward(k_high, 1, EZ)
-
-
-def pack(source, row, target):
-    for j in range(ORDER):
-        target[j * ORDER : j * ORDER + EXTENT] = source[row + j * EXTENT : row + (j + 1) * EXTENT]
-
-
-def add_packed(ref, row, packed):
-    for j in range(ORDER):
-        part = slice(row + j * EXTENT, row + (j + 1) * EXTENT)
-        ref[part] = ref[part] + packed[j * ORDER : j * ORDER + EXTENT]
-    k_low = ref[pl.ds(row, EXTENT, stride=EXTENT), :]
-    ref[pl.ds(row + ORDER, EXTENT, stride=EXTENT), :] = lane_forward(k_low, 1, EZ)
-    ref[row + PLANE - EXTENT : row + PLANE] = lane_forward(ref[row : row + EXTENT], EZ, EY)
-
-
-def expand_packed(ref, row, packed, scale):
-    for j in range(ORDER):
-        ref[row + j * EXTENT : row + (j + 1) * EXTENT] = (
-            scale * packed[j * ORDER : j * ORDER + EXTENT]
-        )
-    spread_lower(ref, row)
-
-
-def spread_lower(ref, row):
-    k_low = ref[pl.ds(row, EXTENT, stride=EXTENT), :]
-    ref[pl.ds(row + ORDER, EXTENT, stride=EXTENT), :] = lane_forward(k_low, 1, EZ)
-    ref[row + PLANE - EXTENT : row + PLANE] = lane_forward(ref[row : row + EXTENT], EZ, EY)
+LOWER = PLANE - EXTENT
+SENT = ORDER * ORDER
+TAIL = LOWER - EXTENT
+
+
+def lines_of(values, count):
+    return [values[j * EXTENT : (j + 1) * EXTENT] for j in range(count)]
+
+
+def sublanes_of(line):
+    return lax.broadcasted_iota(jnp.int32, line.shape, 0)
+
+
+def gather_points(lines, k):
+    rows = sublanes_of(lines[0])
+    points = pltpu.roll(lines[0], (EXTENT - k) % EXTENT, 0) if k else lines[0]
+    for j, line in enumerate(lines):
+        if j:
+            moved = pltpu.roll(line, (j - k) % EXTENT, 0) if (j - k) % EXTENT else line
+            points = jnp.where(rows == j, moved, points)
+    return points
+
+
+def point_at(points, j, k):
+    return pltpu.roll(points, (k - j) % EXTENT, 0) if (k - j) % EXTENT else points
+
+
+def lower_of(values):
+    lines = lines_of(values, EXTENT)
+    lines = [lines[0] + lane_backward(lines[ORDER], EZ, EY)] + lines[1:ORDER]
+    back = lane_backward(gather_points(lines, ORDER), 1, EZ)
+    rows = sublanes_of(back)
+    return [
+        jnp.where(rows == 0, line + point_at(back, j, 0), line) for j, line in enumerate(lines)
+    ]
+
+
+def assembled_of(values):
+    lines = lines_of(values, EXTENT)
+    low = lines[0] + lane_backward(lines[ORDER], EZ, EY)
+    high = lines[ORDER] + lane_forward(lines[0], EZ, EY)
+    lines = [low] + lines[1:ORDER] + [high]
+    back = lane_backward(gather_points(lines, ORDER), 1, EZ)
+    ahead = lane_forward(gather_points(lines, 0), 1, EZ)
+    rows = sublanes_of(back)
+    return [
+        jnp.where(
+            rows == 0,
+            line + point_at(back, j, 0),
+            jnp.where(rows == ORDER, line + point_at(ahead, j, ORDER), line),
+        )
+        for j, line in enumerate(lines)
+    ]
+
+
+def spread_of(lines):
+    ahead = lane_forward(gather_points(lines, 0), 1, EZ)
+    rows = sublanes_of(ahead)
+    lines = [
+        jnp.where(rows == ORDER, point_at(ahead, j, ORDER), line) for j, line in enumerate(lines)
+    ]
+    return lines + [lane_forward(lines[0], EZ, EY)]
+
+
+def plane_of(lines):
+    return jnp.concatenate(lines, axis=0)
+
+
+def store_sent(ref, lines):
+    tail = lines[ORDER - 1]
+    rows = sublanes_of(tail)
+    for j in range(ORDER - 1):
+        ref[j * EXTENT : (j + 1) * EXTENT] = jnp.where(
+            rows == ORDER, point_at(tail, j + 1, ORDER), lines[j]
+        )
+    ref[TAIL:LOWER] = tail
+
+
+def received(packed):
+    tail = packed[pl.ds(ORDER, EXTENT, stride=EXTENT), :]
+    rows = sublanes_of(tail)
+    tail = jnp.where(rows == 0, packed[LOWER : LOWER + EXTENT], tail)
+    return lines_of(packed[EXTENT:LOWER], ORDER - 1) + [tail]
+
+
+def add_lines(one, other):
+    return [a + b for a, b in zip(one, other)]
 
 
 def kernel(
     count, members, groups, scalars_in, transport_in, mass_in, order_in, matrix_in, out,
-    state,    scalars, transport, mass, order, matrix, load_sem, speed, middle, ahead, work, raw, near, far, joint, cross, beyond,
+    state,    scalars, transport, mass, order, matrix, load_sem, speed, middle, ahead, work, raw, joint, cross, beyond,
     mass_send, mass_recv, mass_send_sem, mass_recv_sem,
     coef_send, coef_recv, coef_send_sem, coef_recv_sem, share_send_sem, share_recv_sem,
     send, recv, send_sem, recv_sem,
@@ -198,8 +250,8 @@
     def mass_copies(m):
         return [
             pltpu.make_async_remote_copy(
-                src_ref=mass_send.at[m, side, pl.ds(0, ORDER * ORDER)],
-                dst_ref=mass_recv.at[m, side, pl.ds(0, ORDER * ORDER)],
+                src_ref=mass_send.at[m, side, pl.ds(0, SENT)],
+                dst_ref=mass_recv.at[m, side, pl.ds(EXTENT, SENT)],
                 send_sem=mass_send_sem.at[m, side],
                 recv_sem=mass_recv_sem.at[m, side],
                 device_id=target(side, 1),
@@ -241,8 +293,8 @@
     def face_copies(slot, m, kinds):
         return [
             pltpu.make_async_remote_copy(
-                src_ref=send.at[slot, m, side, kind // 2, pl.ds(0, ORDER * ORDER)],
-                dst_ref=recv.at[slot, m, side, kind, pl.ds(0, ORDER * ORDER)],
+                src_ref=send.at[slot, m, side, kind // 2, pl.ds(0, SENT)],
+                dst_ref=recv.at[slot, m, side, kind, pl.ds(EXTENT, SENT)],
                 send_sem=send_sem.at[slot, m, side, kind],
                 recv_sem=recv_sem.at[slot, m, side, kind],
                 device_id=target(side, 2 if kind == FAR else 1),
@@ -257,6 +309,9 @@
 
     def rows_of(m, i):
         return slice(row_of(m, i), row_of(m, i) + PLANE)
+
+    def lower_rows(m, i):
+        return slice(row_of(m, i), row_of(m, i) + LOWER)
 
     def plane_rows(i):
         return slice(i * PLANE, (i + 1) * PLANE)
@@ -277,19 +332,14 @@
         )
     )
     for side, i in enumerate(ends):
-        store_lower(work, row_of(members, i), block(outer, side))
-        pack(work, row_of(members, i), mass_send.at[members, side])
+        lines = lower_of(block(outer, side))
+        work[lower_rows(members, i), :] = plane_of(lines)
+        store_sent(mass_send.at[members, side], lines)
     for m in range(members):
         for side, i in enumerate(ends):
-            store_lower(
-                work, row_of(m, i), block(outer, side) * block(outer, 2 * (m + 1) + side)
-            )
-            pack(work, row_of(m, i), mass_send.at[m, side])
-    pl.semaphore_wait(barrier, 4 + groups - 1)
-    for m in (members, *range(members)):
-        for copy in mass_copies(m):
-            copy.start()
-
+            lines = lower_of(block(outer, side) * block(outer, 2 * (m + 1) + side))
+            work[lower_rows(m, i), :] = plane_of(lines)
+            store_sent(mass_send.at[m, side], lines)
     loads[3].wait()
     loads[4].wait()
     outer = to_brick(
@@ -299,6 +349,11 @@
         for side, i in enumerate(ends):
             speed[r, plane_rows(i), :] = block(outer, 2 * r + side)
             coef_send[side, plane_rows(r), :] = block(outer, 2 * r + side)
+    pl.semaphore_wait(barrier, 4 + groups - 1)
+    for m in (members, *range(members)):
+        for copy in mass_copies(m):
+            copy.start()
+
     for copy in coef_copies():
         copy.start()
 
@@ -332,8 +387,10 @@
     def take_masses(m):
         for copy in mass_copies(m):
             copy.wait()
-        add_packed(work, row_of(m, 0), mass_recv.at[m, 0])
-        add_packed(work, row_of(m, ORDER), mass_recv.at[m, 1])
+        for side, i in enumerate((0, ORDER)):
+            own = lines_of(work[lower_rows(m, i), :], ORDER)
+            lines = add_lines(own, received(mass_recv.at[m, side]))
+            work[rows_of(m, i), :] = plane_of(spread_of(lines))
 
     take_masses(members)
     scale(0)
@@ -376,17 +433,16 @@
     def first_faces(index, m):
         slot = lax.rem(index, 2)
         for i, value in pair(lambda n: state[slot, rows_of(m, n), :], 0):
-            side = ends.index(i)
-            store_lower(work, row_of(m, i), value)
-            pack(work, row_of(m, i), send.at[slot, m, side, 0])
-        for copy in face_copies(slot, m, (FAR, NEAR)):
+            lines = lower_of(value)
+            store_sent(send.at[slot, m, ends.index(i), 0], lines)
+            work[rows_of(m, i), :] = plane_of(spread_of(lines))
+        for copy in face_copies(slot, m, (NEAR,)):
             copy.start()
 
     def first_inner(index, m):
         slot = lax.rem(index, 2)
         reach, _ = reaches(slot)
         for i in ends:
-            spread_lower(work, row_of(m, i))
             middle[rows_of(m, i), :] = state[0, rows_of(m, i), :] + reach * work[rows_of(m, i), :]
         for a in range(1, half):
             for i, value in pair(lambda n: state[slot, rows_of(m, n), :], a):
@@ -402,9 +458,8 @@
                     across = term if across is None else across + term
             value = speed[0, plane_rows(i), :] * across
             raw[side_rows(m, side), :] = value
-            store_lower(work, row_of(m, i), value)
-            pack(work, row_of(m, i), send.at[slot, m, side, 1])
-        for copy in face_copies(slot, m, (NEXT,)):
+            store_sent(send.at[slot, m, side, 1], lower_of(value))
+        for copy in face_copies(slot, m, (NEXT, FAR)):
             copy.start()
 
     def second_ahead(index, m):
@@ -422,11 +477,11 @@
         for copy in face_copies(slot, m, (NEAR, FAR, NEXT)):
             copy.wait()
         planes = (0, ORDER)
-        for side, i in enumerate(planes):
-            row = (m * 2 + side) * PLANE
-            expand_packed(near, row, recv.at[slot, m, side, NEAR], reach)
-            expand_packed(far, row, recv.at[slot, m, side, FAR], reach)
-        deltas = [near[side_rows(m, side), :] for side in range(2)]
+
+        def taken(side, kind):
+            return spread_of(received(recv.at[slot, m, side, kind]))
+
+        deltas = [reach * plane_of(taken(side, NEAR)) for side in range(2)]
         faces = [middle[rows_of(m, i), :] + deltas[side] for side, i in enumerate(planes)]
         inside = inside_of(faces)
         for side, i in enumerate(planes):
@@ -436,14 +491,12 @@
                 + joint[side, 1] * inside[:PLANE, columns]
                 + joint[side, 2] * inside[PLANE:, columns]
                 + cross[side] * deltas[1 - side]
-                + beyond[side] * far[side_rows(m, side), :]
+                + beyond[side] * (reach * plane_of(taken(side, FAR)))
                 + raw[side_rows(m, 1 - side), :]
             )
-            store_lower(work, row_of(m, i), value)
-            add_packed(work, row_of(m, i), recv.at[slot, m, side, NEXT])
-        for i in planes:
+            total = add_lines(assembled_of(value), taken(side, NEXT))
             state[1 - slot, rows_of(m, i), :] = (
-                state[0, rows_of(m, i), :] + final_reach * work[rows_of(m, i), :]
+                state[0, rows_of(m, i), :] + final_reach * plane_of(total)
             )
         low, high = (final_reach * delta for delta in deltas)
         for i in range(1, ORDER):
@@ -457,11 +510,14 @@
         begin(m, ORDER)
         first_faces(0, m)
         first_inner(0, m)
-
-    for copy in coef_copies():
-        copy.wait()
-    for copy in share_copies():
-        copy.start()
+        if m == 0:
+            for copy in coef_copies():
+                copy.wait()
+            for copy in share_copies():
+                copy.start()
+
+    for m in range(members):
+        second_ahead(0, m)
     for copy in share_copies():
         copy.wait()
     for side, i in enumerate((0, ORDER)):
@@ -475,8 +531,6 @@
         beyond[side] = float(derivative[ORDER - i, i]) * theirs
         for r in (1, 2):
             joint[side, r] = speed[r, plane_rows(i), :] + coef_recv[side, plane_rows(r), :] * inverse
-    for m in range(members):
-        second_ahead(0, m)
 
     def stage(index, carry):
         for m in range(members):
@@ -534,13 +588,11 @@
             floats(members * nodes),
             floats((members + 1) * nodes),
             floats(members * 2 * PLANE),
-            floats(members * 2 * PLANE),
-            floats(members * 2 * PLANE),
             floats(2, 3, PLANE),
             floats(2, PLANE),
             floats(2, PLANE),
-            floats(members + 1, 2, PLANE - EXTENT),
-            floats(members + 1, 2, PLANE - EXTENT),
+            floats(members + 1, 2, PLANE),
+            floats(members + 1, 2, PLANE),
             semaphores(members + 1, 2),
             semaphores(members + 1, 2),
             floats(2, 3 * PLANE),
@@ -549,8 +601,8 @@
             semaphores(2),
             semaphores(groups - 1, 2),
             semaphores(groups - 1, 2),
-            floats(2, members, 2, 2, PLANE - EXTENT),
-            floats(2, members, 2, 3, PLANE - EXTENT),
+            floats(2, members, 2, 2, PLANE),
+            floats(2, members, 2, 3, PLANE),
             semaphores(2, members, 2, 3),
             semaphores(2, members, 2, 3),
         ],

time: 40.9 us -> 38.9 us (0.951)
  Pallas kernels: 40.7 us -> 38.7 us
    pallas_call x1, Pallas kernels: 39.9 us -> 37.9 us  [per_device(): pl.pallas_call(functools.partial(kernel, count, members, groups), out_sha...]
where the time goes in v3:
time: 38.9 us; the launch traced here: 38.8 us
  Pallas kernels  38.7 us (99%)
    pallas_call x1, Pallas kernels, per_device(): pl.pallas_call(functools.partial(kernel, count, members, groups), out_sha...  37.9 us
    pallas_call x1, Pallas kernels, per_device(): pl.pallas_call(store_kernel, out_shape=jax.ShapeDtypeStruct(scalars.shape...  0.8 us

profile of v3, /device:TPU:0, one launch (start us, length us, event | category | flops | bytes accessed | tf_op | source)
XLA Modules:
  0.0 38.8 jit_solution(10311597542934879664)
XLA Ops:
  0.0 37.9 %shard_map.55.result = f32[2,512,128]{2,1,0:T(8,128)S(1)} custom-call(f32[2,512,128]{2,1,0:T(8,128)} %scalars_in.1, f32[3,512,128]{2,1,0:T(8,128)} %transport_in.1, f32[512,128]{1,0:T(8,128)} %mass_in.1, s32[1,128]{1,0:T(1,128)} %order_in.1, bf16[128,192]{1,0:T(8,128)(2,1)} %constant.2.clone.matrix_in), custom_call_target="tpu_custom_call" | custom-call | tf_op jit(solution)/shard_map/pallas_call | solution.py:573
  38.0 0.8 %shard_map.56 = f32[2,512,128]{2,1,0:T(8,128)} custom-call(f32[2,512,128]{2,1,0:T(8,128)S(1)} %shard_map.55.result), custom_call_target="tpu_custom_call" | custom-call | tf_op jit(solution)/shard_map/pallas_call | solution.py:611

commit v4 on v3

--- a/solution.py
+++ b/solution.py
@@ -193,7 +193,7 @@
 
 def kernel(
     count, members, groups, scalars_in, transport_in, mass_in, order_in, matrix_in, out,
-    state,    scalars, transport, mass, order, matrix, load_sem, speed, middle, ahead, work, raw, joint, cross, beyond,
+    state,    scalars, transport, mass, order, matrix, load_sem, speed, bulk, middle, ahead, work, raw, joint, cross, beyond,
     mass_send, mass_recv, mass_send_sem, mass_recv_sem,
     coef_send, coef_recv, coef_send_sem, coef_recv_sem, share_send_sem, share_recv_sem,
     send, recv, send_sem, recv_sem,
@@ -381,6 +381,7 @@
 
     for i in range(1, ORDER):
         scale(i)
+        store_assembled(bulk, i * PLANE, speed[0, plane_rows(i), :])
         for m in range(members):
             begin(m, i)
 
@@ -393,8 +394,9 @@
             work[rows_of(m, i), :] = plane_of(spread_of(lines))
 
     take_masses(members)
-    scale(0)
-    scale(ORDER)
+    for i in (0, ORDER):
+        scale(i)
+        bulk[plane_rows(i), :] = plane_of(assembled_of(speed[0, plane_rows(i), :]))
 
     derivative = gll_derivative(ORDER)
     half = EXTENT // 2
@@ -456,9 +458,9 @@
                 if n != i:
                     term = float(derivative[i, n]) * middle[rows_of(m, n), :]
                     across = term if across is None else across + term
-            value = speed[0, plane_rows(i), :] * across
+            value = bulk[plane_rows(i), :] * across
             raw[side_rows(m, side), :] = value
-            store_sent(send.at[slot, m, side, 1], lower_of(value))
+            store_sent(send.at[slot, m, side, 1], lines_of(value, ORDER))
         for copy in face_copies(slot, m, (NEXT, FAR)):
             copy.start()
 
@@ -474,7 +476,7 @@
     def second(index, m):
         slot = lax.rem(index, 2)
         reach, final_reach = reaches(slot)
-        for copy in face_copies(slot, m, (NEAR, FAR, NEXT)):
+        for copy in face_copies(slot, m, (NEAR,)):
             copy.wait()
         planes = (0, ORDER)
 
@@ -486,23 +488,35 @@
         inside = inside_of(faces)
         for side, i in enumerate(planes):
             columns = slice(side * elements, (side + 1) * elements)
-            value = (
-                joint[side, 0] * faces[side]
-                + joint[side, 1] * inside[:PLANE, columns]
+            within_plane = assembled_of(
+                joint[side, 1] * inside[:PLANE, columns]
                 + joint[side, 2] * inside[PLANE:, columns]
+            )
+            total = (
+                plane_of(within_plane)
+                + joint[side, 0] * faces[side]
                 + cross[side] * deltas[1 - side]
-                + beyond[side] * (reach * plane_of(taken(side, FAR)))
                 + raw[side_rows(m, 1 - side), :]
             )
-            total = add_lines(assembled_of(value), taken(side, NEXT))
-            state[1 - slot, rows_of(m, i), :] = (
-                state[0, rows_of(m, i), :] + final_reach * plane_of(total)
-            )
+            work[rows_of(m, i), :] = state[0, rows_of(m, i), :] + final_reach * total
         low, high = (final_reach * delta for delta in deltas)
         for i in range(1, ORDER):
             across = float(derivative[i, 0]) * low + float(derivative[i, ORDER]) * high
-            store_assembled(work, row_of(m, i), speed[0, plane_rows(i), :] * across)
-            state[1 - slot, rows_of(m, i), :] = ahead[rows_of(m, i), :] + work[rows_of(m, i), :]
+            state[1 - slot, rows_of(m, i), :] = (
+                ahead[rows_of(m, i), :] + bulk[plane_rows(i), :] * across
+            )
+        for copy in face_copies(slot, m, (NEXT, FAR)):
+            copy.wait()
+        for side, i in enumerate(planes):
+            lines = [
+                final_reach * (after + weight * (reach * away))
+                for after, weight, away in zip(
+                    received(recv.at[slot, m, side, NEXT]),
+                    lines_of(beyond[side], ORDER),
+                    received(recv.at[slot, m, side, FAR]),
+                )
+            ]
+            state[1 - slot, rows_of(m, i), :] = work[rows_of(m, i), :] + plane_of(spread_of(lines))
 
     for m in range(members):
         take_masses(m)
@@ -522,8 +536,8 @@
         copy.wait()
     for side, i in enumerate((0, ORDER)):
         inverse = -time_step * work[rows_of(members, i), :]
-        theirs = coef_recv[side, plane_rows(0), :] * inverse
-        ours = speed[0, plane_rows(i), :]
+        theirs = plane_of(assembled_of(coef_recv[side, plane_rows(0), :] * inverse))
+        ours = bulk[plane_rows(i), :]
         joint[side, 0] = float(derivative[i, i]) * ours + (
             float(derivative[ORDER - i, ORDER - i]) * theirs
         )
@@ -584,6 +598,7 @@
             pltpu.VMEM(matrix.shape, matrix.dtype),
             semaphores(5),
             floats(3, nodes),
+            floats(nodes),
             floats(members * nodes),
             floats(members * nodes),
             floats((members + 1) * nodes),

time: 38.9 us -> 37.9 us (0.974)
  Pallas kernels: 38.7 us -> 37.7 us
    pallas_call x1, Pallas kernels: 37.9 us -> 36.9 us  [per_device(): pl.pallas_call(functools.partial(kernel, count, members, groups), out_sha...]
where the time goes in v4:
time: 37.9 us; the launch traced here: 37.7 us
  Pallas kernels  37.7 us (99%)
    pallas_call x1, Pallas kernels, per_device(): pl.pallas_call(functools.partial(kernel, count, members, groups), out_sha...  36.9 us
    pallas_call x1, Pallas kernels, per_device(): pl.pallas_call(store_kernel, out_shape=jax.ShapeDtypeStruct(scalars.shape...  0.8 us

profile of v4, /device:TPU:0, one launch (start us, length us, event | category | flops | bytes accessed | tf_op | source)
XLA Modules:
  0.0 37.7 jit_solution(1159358776783145035)
XLA Ops:
  0.0 36.9 %shard_map.55.result = f32[2,512,128]{2,1,0:T(8,128)S(1)} custom-call(f32[2,512,128]{2,1,0:T(8,128)} %scalars_in.1, f32[3,512,128]{2,1,0:T(8,128)} %transport_in.1, f32[512,128]{1,0:T(8,128)} %mass_in.1, s32[1,128]{1,0:T(1,128)} %order_in.1, bf16[128,192]{1,0:T(8,128)(2,1)} %constant.2.clone.matrix_in), custom_call_target="tpu_custom_call" | custom-call | tf_op jit(solution)/shard_map/pallas_call | solution.py:587
  36.9 0.8 %shard_map.56 = f32[2,512,128]{2,1,0:T(8,128)} custom-call(f32[2,512,128]{2,1,0:T(8,128)S(1)} %shard_map.55.result), custom_call_target="tpu_custom_call" | custom-call | tf_op jit(solution)/shard_map/pallas_call | solution.py:626

commit v5 on v4

--- a/solution.py
+++ b/solution.py
@@ -276,7 +276,7 @@
             for side in sides
         ]
 
-    def share_copies():
+    def share_copies(places):
         return [
             pltpu.make_async_remote_copy(
                 src_ref=coef_recv.at[side, shared],
@@ -287,7 +287,7 @@
                 device_id_type=MESH,
             )
             for distance in range(1, groups)
-            for side in sides
+            for side in (sides[place] for place in places)
         ]
 
     def face_copies(slot, m, kinds):
@@ -520,19 +520,22 @@
 
     for m in range(members):
         take_masses(m)
+        if m == 0:
+            coef_copies()[1].wait()
+            for copy in share_copies((1,)):
+                copy.start()
         begin(m, 0)
         begin(m, ORDER)
         first_faces(0, m)
         first_inner(0, m)
         if m == 0:
-            for copy in coef_copies():
-                copy.wait()
-            for copy in share_copies():
+            coef_copies()[0].wait()
+            for copy in share_copies((0,)):
                 copy.start()
 
     for m in range(members):
         second_ahead(0, m)
-    for copy in share_copies():
+    for copy in share_copies((0, 1)):
         copy.wait()
     for side, i in enumerate((0, ORDER)):
         inverse = -time_step * work[rows_of(members, i), :]

time: 37.9 us -> 37.9 us (level)
  no operation moved by 1% of the time
where the time goes in v5:
time: 37.9 us; the launch traced here: 37.8 us
  Pallas kernels  37.7 us (99%)
    pallas_call x1, Pallas kernels, per_device(): pl.pallas_call(functools.partial(kernel, count, members, groups), out_sha...  36.9 us
    pallas_call x1, Pallas kernels, per_device(): pl.pallas_call(store_kernel, out_shape=jax.ShapeDtypeStruct(scalars.shape...  0.8 us

profile of v5, /device:TPU:0, one launch (start us, length us, event | category | flops | bytes accessed | tf_op | source)
XLA Modules:
  0.0 37.8 jit_solution(9482632772314805165)
XLA Ops:
  0.0 36.9 %shard_map.55.result = f32[2,512,128]{2,1,0:T(8,128)S(1)} custom-call(f32[2,512,128]{2,1,0:T(8,128)} %scalars_in.1, f32[3,512,128]{2,1,0:T(8,128)} %transport_in.1, f32[512,128]{1,0:T(8,128)} %mass_in.1, s32[1,128]{1,0:T(1,128)} %order_in.1, bf16[128,192]{1,0:T(8,128)(2,1)} %constant.2.clone.matrix_in), custom_call_target="tpu_custom_call" | custom-call | tf_op jit(solution)/shard_map/pallas_call | solution.py:590
  36.9 0.8 %shard_map.56 = f32[2,512,128]{2,1,0:T(8,128)} custom-call(f32[2,512,128]{2,1,0:T(8,128)S(1)} %shard_map.55.result), custom_call_target="tpu_custom_call" | custom-call | tf_op jit(solution)/shard_map/pallas_call | solution.py:629
